TPU v7x, 32 devices: a whole 2x2x4 slice. The times are simulated.
32 devices in a mesh: layer: 4 (over x, core), tok: 8 (over z, y).
Axes of the slice: x: 2, y: 2, z: 4, core: 2. Of those that a mesh axis runs over, the one named last changes fastest.
Arguments:
- kv_cache: bfloat16 [4, 2, 2, 1, 1024, 1024], P('layer', None, None, None, 'tok'), may hold values from -6 to 6
- keep_mask: int32 [4, 1, 1024], P('layer', None, 'tok'), may hold values 0 or 1
- lengths: int32 [1], replicated, may hold values from 256 to 1024
Outputs:
- decode_cache: bfloat16 [1, 8, 8, 2, 1024, 128], P(None, 'layer', None, None, 'tok')
Inputs may be any that keep to these rules, and one draw needn't show every extreme that they name: `keep_mask`: 1 keeps the token of both layers of the pair unmerged. `lengths`: positions at or past a sequence's length are padding.
All inputs are finite; a program needn't handle non-finite values. No bound on the sum of `keep_mask` on one device may be relied on, other than what follows from the above.
Results may differ from a plain program's by a relative error of at most 0.001.
Values may be sent and summed in bfloat16 or wider, within the bound.
No kernel may reach another device: no remote copies, remote signals or barrier semaphores. Data moves between devices by JAX's collectives and lax.ppermute only.
A program may use at most 64 MiB of HBM per device.

v0:
```python
import jax
import jax.numpy as jnp
from jax import lax
from jax.sharding import PartitionSpec as P

KVH = 8
HD = 128
PAGE = 16


epsilon = 1e-06


def merge_pair(lower_layer, upper_layer, retained, inside):
    lower_scale = jnp.sqrt(jnp.mean(lower_layer * lower_layer, axis=-1, keepdims=True) + epsilon)
    upper_scale = jnp.sqrt(jnp.mean(upper_layer * upper_layer, axis=-1, keepdims=True) + epsilon)
    summed = lower_layer / lower_scale + upper_layer / upper_scale
    direction = summed / jnp.sqrt(jnp.mean(summed * summed, axis=-1, keepdims=True) + epsilon)
    lower_out = jnp.where(retained, lower_layer, lower_scale * direction)
    upper_out = jnp.where(retained, upper_layer, upper_scale * direction)
    lower_out = jnp.where(inside, lower_out, jnp.zeros_like(lower_out))
    upper_out = jnp.where(inside, upper_out, jnp.zeros_like(upper_out))
    return jnp.stack([lower_out, upper_out], axis=0).astype(jnp.bfloat16)


def shards(kv_cache, keep_mask, lengths):
    groups = lax.axis_size("layer")
    tok_count = lax.axis_size("tok")
    seq_count = kv_cache.shape[3]
    rows_dev = kv_cache.shape[4]
    head_group = KVH // groups
    round_group = rows_dev // (PAGE * tok_count)
    offset = lax.axis_index("tok") * rows_dev
    position = offset + jnp.arange(rows_dev, dtype=jnp.int32)
    inside = (position[None, :] < lengths[:, None])[None, :, :, None, None]
    retained = (keep_mask[0] > 0)[None, :, :, None, None]
    values = kv_cache[0].astype(jnp.float32).reshape(2, 2, seq_count, rows_dev, KVH, HD)
    merged = merge_pair(values[0], values[1], retained, inside)
    outgoing = merged.reshape(2, 2, seq_count, round_group, tok_count, PAGE, groups, head_group, HD)
    outgoing = outgoing.transpose(6, 4, 2, 7, 0, 1, 3, 5, 8)
    flat = outgoing.reshape((groups * tok_count,) + outgoing.shape[2:])
    arrived = lax.all_to_all(
        flat, ("layer", "tok"), split_axis=0, concat_axis=0, tiled=True
    ).reshape(outgoing.shape)
    result = arrived.transpose(2, 3, 0, 4, 5, 1, 6, 7, 8)
    return result.reshape(seq_count, head_group, 2 * groups, 2, rows_dev, HD)


def solution(mesh):
    in_specs = (P("layer", None, None, None, "tok", None), P("layer", None, "tok"), P())
    out_specs = P(None, "layer", None, None, "tok", None)
    return jax.shard_map(shards, mesh=mesh, in_specs=in_specs, out_specs=out_specs, check_vma=False)
```

profile of v0, /device:TPU:0, one launch (start us, length us, event | category | flops | bytes accessed | tf_op | source)
XLA Modules:
  0.0 60.9 jit_solution(14632242213081698285)
XLA Ops:
  0.0 1.4 %fusion.7 = (f32[1,1,2,1,128,1024]{5,4,3,2,1,0:T(8,128)S(1)}, f32[1,1,2,1,128,1024]{5,4,3,2,1,0:T(8,128)S(1)}) fusion(bf16[1,2,2,1,128,1024]{5,4,3,2,1,0:T(8,128)(2,1)} %param.3), kind=kLoop, calls=%fused_computation.19 | loop fusion | bytes 4194304 | tf_op jit(solution)/shard_map/slice | solution.py:38
  1.4 0.0 copy-start.1
  1.5 0.0 copy-start
  1.5 0.2 copy.59
  1.7 0.8 %copy-done.1 = f32[1,1,2,1,128,1024]{5,4,3,2,1,0:T(8,128)} copy-done((f32[1,1,2,1,128,1024]{5,4,3,2,1,0:T(8,128)}, f32[1,1,2,1,128,1024]{5,4,3,2,1,0:T(8,128)S(1)}, u32[]{:S(2)}) %copy-start.1) | copy-done | bytes 1048600
  2.4 0.3 multiply_reduce_fusion.1
  2.8 0.1 copy.43
  2.9 0.1 copy.47
  3.0 0.7 %sqrt.39 = f32[2,8,16,4,2]{2,1,4,3,0:T(8,128)} reshape(f32[2,128,8]{1,2,0:T(8,128)S(1)} %add_sqrt_fusion.1) | data formatting | bytes 16384 | tf_op jit(solution)/shard_map/sqrt | solution.py:16
  3.7 0.0 copy-done
  3.7 0.2 copy.58
  3.9 0.3 multiply_reduce_fusion.2
  4.3 0.1 copy.40
  4.3 0.1 copy.46
  4.5 0.7 %sqrt.37 = f32[2,8,16,4,2]{2,1,4,3,0:T(8,128)} reshape(f32[2,128,8]{1,2,0:T(8,128)S(1)} %add_sqrt_fusion.2) | data formatting | bytes 16384 | tf_op jit(solution)/shard_map/sqrt | solution.py:15
  5.2 2.1 %squeeze.14 = f32[1,2,8,16,4,2,128]{6,5,4,0,3,2,1:T(2,128)S(1)} reshape(f32[1,1,2,1,128,1024]{5,4,3,2,1,0:T(8,128)} %copy-done.1) | data formatting | bytes 2097152 | tf_op jit(solution)/shard_map/squeeze | solution.py:38
  7.3 3.1 %squeeze.12 = f32[1,2,8,16,4,2,128]{6,5,4,0,3,2,1:T(2,128)} reshape(f32[1,1,2,1,128,1024]{5,4,3,2,1,0:T(8,128)} %copy-done) | data formatting | bytes 2097152 | tf_op jit(solution)/shard_map/squeeze | solution.py:38
  10.4 1.0 %multiply_reduce_fusion = f32[2,128,8]{2,1,0:T(8,128)S(1)} fusion(f32[2,1,128,8,128]{4,3,2,0,1:T(8,128)S(1)} %bitcast.75, f32[2,1,128,8,128]{4,3,2,0,1:T(8,128)S(1)} %bitcast.77, f32[2,128,8]{2,1,0:T(8,128)S(1)} %copy.47, f32[2,128,8]{2,1,0:T(8,128)S(1)} %copy.46), kind=kLoop, calls=%fused_computation.8 | loop fusion | flops 1308672 | bytes 2121728 | tf_op jit(solution)/shard_map/reduce_sum | solution.py:18
  11.4 0.0 copy-start.2
  11.4 0.1 copy.48
  11.5 0.1 sqrt.41
  11.6 0.5 copy.49
  12.1 1.3 %copy.44 = f32[2,8,16,4,2]{4,3,2,1,0:T(4,128)S(1)} copy(f32[2,8,16,4,2]{2,1,4,3,0:T(8,128)} %sqrt.39) | data formatting | bytes 16384 | tf_op jit(solution)/shard_map/sqrt | solution.py:16
  13.4 0.0 copy-done.3
  13.4 1.2 %copy.41 = f32[2,8,16,4,2]{4,3,2,1,0:T(4,128)} copy(f32[2,8,16,4,2]{2,1,4,3,0:T(8,128)S(1)} %copy-done.3) | data formatting | bytes 16384 | tf_op jit(solution)/shard_map/sqrt | solution.py:15
  15.3 0.1 gt.18
  15.4 6.0 %fusion.5 = (bf16[1,2,1,1,8,16,4,2,128]{8,7,6,5,4,1,3,2,0:T(2,128)(2,1)S(1)}, f32[1,2,8,16,4,2,128]{6,5,4,3,2,1,0:T(2,128)S(1)}) fusion(f32[1,2,8,16,4,2,128]{6,5,4,0,3,2,1:T(2,128)S(1)} %copy-done.2, f32[2,8,16,4,2]{4,3,2,1,0:T(4,128)} %copy.41, pred[8,16]{1,0:T(8,128)(4,1)S(1)} %gt.18, pred[8,16]{1,0:T(8,128)(4,1)S(1)} %add_compare_fusion, ...), kind=kLoop, calls=%fused_computation.13 | loop fusion | flops 1835008 | bytes 3694848 | tf_op jit(solution)/shard_map/stack | solution.py:23
  21.5 1.8 %fusion.4 = bf16[1,2,1,1,8,16,4,2,128]{8,7,6,5,4,1,3,2,0:T(2,128)(2,1)S(1)} fusion(f32[1,2,8,16,4,2,128]{6,5,4,3,2,1,0:T(2,128)S(1)} %get-tuple-element.6, f32[2,8,16,4,2]{4,3,2,1,0:T(4,128)S(1)} %copy.44, f32[1,2,8,16,4,2,128]{6,5,4,0,3,2,1:T(2,128)S(1)} %squeeze.14, pred[8,16]{1,0:T(8,128)(4,1)S(1)} %gt.18, pred[8,16]{1,0:T(8,128)(4,1)S(1)} %add_compare_fusion), kind=kLoop, calls=%fused_computation.12 | loop fusion | flops 786432 | bytes 2629888 | tf_op jit(solution)/shard_map/stack | solution.py:23
  23.3 1.5 %maximum_bitcast_fusion = bf16[4,8,1,2,2,2,1,16,128]{8,3,0,7,1,5,6,2,4:T(2,128)(2,1)S(1)} fusion(bf16[1,2,1,1,8,16,4,2,128]{8,7,6,5,4,1,3,2,0:T(2,128)(2,1)S(1)} %fusion.4, bf16[1,2,1,1,8,16,4,2,128]{8,7,6,5,4,1,3,2,0:T(2,128)(2,1)S(1)} %get-tuple-element.5), kind=kLoop, calls=%fused_computation.4 | loop fusion | flops 524288 | bytes 2097152 | tf_op jit(solution)/shard_map/transpose | solution.py:40
  24.8 0.3 copy.55
  25.1 34.6 %all_to_all.5 = bf16[32,1,2,2,2,1,16,128]{7,6,4,3,2,5,1,0:T(8,128)(2,1)S(1)} all-to-all(bf16[32,1,2,2,2,1,16,128]{7,6,4,3,2,5,1,0:T(8,128)(2,1)S(1)} %bitcast.80), channel_id=1, replica_groups=mesh['layer'=4,'tok'=8] {'layer','tok'}, dimensions={0} | all-to-all | bytes 2097152 | tf_op jit(solution)/shard_map/all_to_all | solution.py:42
  59.7 1.2 %copy.57 = bf16[1,2,4,2,2,8,1,16,128]{8,7,5,4,3,2,1,6,0:T(8,128)(2,1)} copy(bf16[1,2,4,2,2,8,1,16,128]{8,7,4,3,1,5,2,6,0:T(8,128)(2,1)S(1)} %bitcast.81) | data formatting | bytes 2097152 | tf_op jit(solution)/shard_map/transpose | solution.py:45
  (9 shorter events, 0.1 us)
Async XLA Ops:
  1.4 1.0 %copy-start.1 = (f32[1,1,2,1,128,1024]{5,4,3,2,1,0:T(8,128)}, f32[1,1,2,1,128,1024]{5,4,3,2,1,0:T(8,128)S(1)}, u32[]{:S(2)}) copy-start(f32[1,1,2,1,128,1024]{5,4,3,2,1,0:T(8,128)S(1)} %get-tuple-element.7) | copy-start | bytes 3145732
  1.5 2.3 %copy-start = (f32[1,1,2,1,128,1024]{5,4,3,2,1,0:T(8,128)}, f32[1,1,2,1,128,1024]{5,4,3,2,1,0:T(8,128)S(1)}, u32[]{:S(2)}) copy-start(f32[1,1,2,1,128,1024]{5,4,3,2,1,0:T(8,128)S(1)} %get-tuple-element.8) | copy-start | bytes 3145732
  11.4 4.0 %copy-start.2 = (f32[1,2,8,16,4,2,128]{6,5,4,0,3,2,1:T(2,128)S(1)}, f32[1,2,8,16,4,2,128]{6,5,4,0,3,2,1:T(2,128)}, u32[]{:S(2)}) copy-start(f32[1,2,8,16,4,2,128]{6,5,4,0,3,2,1:T(2,128)} %squeeze.12) | copy-start | bytes 3145732
  12.1 1.3 %copy-start.3 = (f32[2,8,16,4,2]{2,1,4,3,0:T(8,128)S(1)}, f32[2,8,16,4,2]{2,1,4,3,0:T(8,128)}, u32[]{:S(2)}) copy-start(f32[2,8,16,4,2]{2,1,4,3,0:T(8,128)} %sqrt.37) | copy-start | bytes 24580
  14.6 0.7 %copy-start.4 = (s32[1,1,128]{2,1,0:T(1,128)S(1)}, s32[1,1,128]{2,1,0:T(1,128)}, u32[]{:S(2)}) copy-start(s32[1,1,128]{2,1,0:T(1,128)} %param.4) | copy-start | bytes 1540
where the time goes:
time: 61.5 us; the launch traced here: 60.9 us
  blocking collectives  34.6 us (56%)
  local copies, waits for them, and re-layouts  14.4 us (23%)
  other arithmetic  11.1 us (18%)
  between operations  0.83 us (1%)
    all_to_all x1, blocking collectives, shards(): lax.all_to_all(flat, ('layer', 'tok'), split_axis=0, concat_axis=0, tiled...  34.6 us
    another operation x2, other arithmetic, merge_pair(): return jnp.stack([lower_out, upper_out], axis=0).astype(jnp.bfloat16)  7.87 us
    squeeze x2, local copies, waits for them, and re-layouts, shards(): merged = merge_pair(values[0], values[1], retained, inside)  5.22 us
    sqrt x3, local copies, waits for them, and re-layouts, merge_pair(): jnp.sqrt(jnp.mean(upper_layer * upper_layer, axis=-1, keepdims=True) + ep...  2.16 us
    sqrt x3, local copies, waits for them, and re-layouts, merge_pair(): jnp.sqrt(jnp.mean(lower_layer * lower_layer, axis=-1, keepdims=True) + ep...  2.09 us
    transpose x1, other arithmetic, shards(): outgoing = outgoing.transpose(6, 4, 2, 7, 0, 1, 3, 5, 8)  1.48 us
    slice x1, local copies, waits for them, and re-layouts, shards(): merged = merge_pair(values[0], values[1], retained, inside)  1.43 us
    transpose x1, local copies, waits for them, and re-layouts, shards(): result = arrived.transpose(2, 3, 0, 4, 5, 1, 6, 7, 8)  1.24 us

commit v1 on v0

v1 whole, which is shorter than its diff:
```python
import functools

import jax
import jax.numpy as jnp
from jax import lax
from jax.experimental import pallas as pl
from jax.experimental.pallas import tpu as pltpu
from jax.sharding import PartitionSpec as P

KVH = 8
HD = 128
PAGE = 16


epsilon = 1e-06


def column(row, rows):
    parts = [
        jnp.broadcast_to(row[:, k : k + HD], (HD, HD)).T for k in range(0, rows, HD)
    ]
    return parts[0] if len(parts) == 1 else jnp.concatenate(parts, axis=0)


def merge_kernel(first_ref, length_ref, keep_ref, values_ref, out_ref, *, head_group):
    rows = values_ref.shape[2]
    pages = rows // PAGE
    keep = column((keep_ref[...] > 0).astype(jnp.float32), rows)
    position = first_ref[0] + lax.broadcasted_iota(jnp.int32, (rows, HD), 0)
    inside = position < length_ref[0]
    retained = jnp.logical_and(keep > 0.0, inside)
    live = inside.astype(jnp.float32)
    for head in range(KVH):
        lanes = slice(head * HD, (head + 1) * HD)
        lower = values_ref[0, 0, :, lanes].astype(jnp.float32)
        upper = values_ref[1, 0, :, lanes].astype(jnp.float32)
        lower_square = jnp.mean(lower * lower, axis=-1, keepdims=True) + epsilon
        upper_square = jnp.mean(upper * upper, axis=-1, keepdims=True) + epsilon
        lower_inverse = lax.rsqrt(lower_square)
        upper_inverse = lax.rsqrt(upper_square)
        summed = lower * lower_inverse + upper * upper_inverse
        summed_inverse = lax.rsqrt(jnp.mean(summed * summed, axis=-1, keepdims=True) + epsilon)
        direction = summed * (summed_inverse * live)
        lower_out = jnp.where(retained, lower, (lower_square * lower_inverse) * direction)
        upper_out = jnp.where(retained, upper, (upper_square * upper_inverse) * direction)
        group, member = head // head_group, head % head_group
        out_ref[group, :, member, 0, 0] = lower_out.astype(jnp.bfloat16).reshape(pages, PAGE, HD)
        out_ref[group, :, member, 1, 0] = upper_out.astype(jnp.bfloat16).reshape(pages, PAGE, HD)


def merged_pages(values, keep, lengths, first, groups):
    rows = values.shape[2]
    head_group = KVH // groups
    pages = rows // PAGE
    return pl.pallas_call(
        functools.partial(merge_kernel, head_group=head_group),
        grid=(2,),
        in_specs=[
            pl.BlockSpec(memory_space=pltpu.SMEM),
            pl.BlockSpec(memory_space=pltpu.SMEM),
            pl.BlockSpec((1, rows), lambda c: (0, 0)),
            pl.BlockSpec((2, 1, rows, KVH * HD), lambda c: (0, c, 0, 0)),
        ],
        out_specs=pl.BlockSpec(
            (groups, pages, head_group, 2, 1, PAGE, HD), lambda c: (0, 0, 0, 0, c, 0, 0)
        ),
        out_shape=jax.ShapeDtypeStruct(
            (groups, pages, head_group, 2, 2, PAGE, HD), jnp.bfloat16
        ),
    )(first, lengths, keep, values)


def shards(kv_cache, keep_mask, lengths):
    groups = lax.axis_size("layer")
    tok_count = lax.axis_size("tok")
    seq_count = kv_cache.shape[3]
    rows_dev = kv_cache.shape[4]
    head_group = KVH // groups
    rounds = rows_dev // (PAGE * tok_count)
    first = (lax.axis_index("tok") * rows_dev).astype(jnp.int32).reshape(1)
    pieces = []
    for s in range(seq_count):
        pages = merged_pages(
            kv_cache[0, :, :, s], keep_mask[0, s : s + 1], lengths[s : s + 1], first, groups
        )
        pages = pages.reshape(groups, rounds, tok_count, -1)
        pieces.append(pages.transpose(0, 2, 1, 3))
    outgoing = jnp.stack(pieces, axis=2)
    shape = (groups, tok_count, seq_count, rounds, head_group, 2, 2, PAGE, HD)
    flat = outgoing.reshape((groups * tok_count, -1) + shape[-2:])
    arrived = lax.all_to_all(
        flat, ("layer", "tok"), split_axis=0, concat_axis=0, tiled=True
    ).reshape(shape)
    result = arrived.transpose(2, 4, 0, 5, 6, 1, 3, 7, 8)
    return result.reshape(seq_count, head_group, 2 * groups, 2, rows_dev, HD)


def solution(mesh):
    in_specs = (P("layer", None, None, None, "tok", None), P("layer", None, "tok"), P())
    out_specs = P(None, "layer", None, None, "tok", None)
    return jax.shard_map(shards, mesh=mesh, in_specs=in_specs, out_specs=out_specs, check_vma=False)
```

time: 61.5 us -> 40.8 us (0.66)
  local copies, waits for them, and re-layouts: 14.4 us -> 1.24 us
  other arithmetic: 11.1 us -> 0 us
  Pallas kernels: 0 us -> 3.87 us
    another operation x2 -> x0, other arithmetic: 7.87 us -> none  [merge_pair(): return jnp.stack([lower_out, upper_out], axis=0).astype(jnp.bfloat16)]
    squeeze x2 -> x0, local copies, waits for them, and re-layouts: 5.22 us -> none  [shards(): merged = merge_pair(values[0], values[1], retained, inside)]
    sqrt x8 -> x0, local copies, waits for them, and re-layouts: 4.8 us -> none  [the longest x3 2.16 us: merge_pair(): jnp.sqrt(jnp.mean(upper_layer * upper_layer, axis=-1, keepdims=True) + ep...]
    pallas_call x0 -> x1, Pallas kernels: none -> 3.87 us  [merged_pages(): pl.pallas_call(functools.partial(merge_kernel, head_group=head_group), gr...]
    reduce_sum x3 -> x0, other arithmetic: 1.69 us -> none  [the longest x1 1.01 us: merge_pair(): jnp.mean(summed * summed, axis=-1, keepdims=True) + epsilon]
    transpose x2 -> x0, local copies, waits for them, and re-layouts: 1.49 us -> none  [the longest x1 1.24 us: shards(): result = arrived.transpose(2, 3, 0, 4, 5, 1, 6, 7, 8)]
    transpose x1 -> x0, other arithmetic: 1.48 us -> none  [shards(): outgoing = outgoing.transpose(6, 4, 2, 7, 0, 1, 3, 5, 8)]
    slice x1 -> x0, local copies, waits for them, and re-layouts: 1.43 us -> none  [shards(): merged = merge_pair(values[0], values[1], retained, inside)]
where the time goes in v1:
time: 40.8 us; the launch traced here: 40.6 us
  blocking collectives  34.8 us (85%)
  Pallas kernels  3.87 us (9%)
  local copies, waits for them, and re-layouts  1.24 us (3%)
  between operations  0.65 us (2%)
    all_to_all x1, blocking collectives, shards(): lax.all_to_all(flat, ('layer', 'tok'), split_axis=0, concat_axis=0, tiled...  34.8 us
    pallas_call x1, Pallas kernels, merged_pages(): pl.pallas_call(functools.partial(merge_kernel, head_group=head_group), gr...  3.87 us
    reshape x1, local copies, waits for them, and re-layouts, shards(): arrived = lax.all_to_all(flat, ('layer', 'tok'), split_axis=0, concat_axi...  1.24 us

profile of v1, /device:TPU:0, one launch (start us, length us, event | category | flops | bytes accessed | tf_op | source)
XLA Modules:
  0.0 40.6 jit_solution(3632752323258609321)
XLA Ops:
  0.7 3.9 %shard_map.37 = bf16[4,8,2,2,2,16,128]{6,5,4,3,2,1,0:T(8,128)(2,1)} custom-call(s32[1]{0:T(128)} %bitcast.first_ref, s32[1]{0:T(128)S(6)} %copy.5.length_ref, s32[1,128]{1,0:T(1,128)} %bitcast.11, bf16[2,2,128,1024]{3,2,1,0:T(8,128)(2,1)} %bitcast.10), custom_call_target="tpu_custom_call" | custom-call | tf_op jit(solution)/shard_map/pallas_call | solution.py:55
  4.5 34.8 %all_to_all.5 = bf16[32,8,16,128]{3,2,1,0:T(8,128)(2,1)S(1)} all-to-all(bf16[32,8,16,128]{3,2,1,0:T(8,128)(2,1)} %bitcast.8), channel_id=1, replica_groups=mesh['layer'=4,'tok'=8] {'layer','tok'}, dimensions={0} | all-to-all | bytes 2097152 | tf_op jit(solution)/shard_map/all_to_all | solution.py:91
  39.3 1.2 %copy.4 = bf16[4,8,1,1,2,2,2,16,128]{8,7,1,6,5,0,4,3,2:T(8,128)(2,1)} copy(bf16[4,8,1,1,2,2,2,16,128]{8,7,6,5,4,1,0,3,2:T(8,128)(2,1)S(1)} %bitcast.9) | data formatting | bytes 2097152 | tf_op jit(solution)/shard_map/reshape | solution.py:93
